TPU v7x, 32 devices: a whole 2x2x4 slice. The times are simulated.
32 devices in a mesh: seg: 4 (over z), ch: 8 (over y, x, core).
Axes of the slice: x: 2, y: 2, z: 4, core: 2. Of those that a mesh axis runs over, the one named last changes fastest.
Arguments:
- gate_in: bfloat16 [1536, 16384], P('ch', 'seg'), may hold values from -6 to 6
- key_in: bfloat16 [1536, 16384], P('ch', 'seg'), may hold values from -6 to 6
- value_in: bfloat16 [1536, 16384], P('ch', 'seg'), may hold values from -6 to 6
- kernel: float32 [1536, 16384], P('ch'), may hold values from -0.046875 to 0.046875
- skip_gain: float32 [1536], P('ch'), may hold values from -1 to 1
- out_weight: bfloat16 [1536, 1536], P('ch'), may hold values from -0.15625 to 0.15625
Outputs:
- output: bfloat16 [16384, 1536], P(('seg', 'ch'))
All inputs are finite; a program needn't handle non-finite values.
Results may differ from a plain program's by a relative error of at most 0.0095.
Values may be sent and summed in bfloat16 or wider, within the bound.
A program may use at most 128 MiB of HBM per device.

v0:
```python
import math

import jax
import jax.numpy as jnp
from jax import lax
from jax.sharding import PartitionSpec as P

lane_width = 128
highest = lax.Precision.HIGHEST


def angle_pair(height, breadth, period):
    product = (
        jnp.arange(height, dtype=jnp.int32)[:, None]
        * jnp.arange(breadth, dtype=jnp.int32)[None, :]
        % period
    )
    theta = product.astype(jnp.float32) * (2.0 * math.pi / period)
    return (jnp.cos(theta), jnp.sin(theta))


def make_tables(outer):
    cos_outer, sin_outer = angle_pair(outer, outer, outer)
    cos_inner, sin_inner = angle_pair(lane_width, lane_width, lane_width)
    cos_twist, sin_twist = angle_pair(outer, lane_width, outer * lane_width)
    return (cos_outer, sin_outer, cos_inner, sin_inner, cos_twist, sin_twist)


def left_mul(matrix, stack):
    return jnp.einsum("kn,cnm->ckm", matrix, stack, precision=highest)


def right_mul(stack, matrix):
    return jnp.einsum("ckn,nm->ckm", stack, matrix, precision=highest)


def forward(signal, tables):
    cos_outer, sin_outer, cos_inner, sin_inner, cos_twist, sin_twist = tables
    height = signal.shape[1]
    real_a = left_mul(cos_outer[:, :height], signal)
    imag_a = -left_mul(sin_outer[:, :height], signal)
    real_b = real_a * cos_twist + imag_a * sin_twist
    imag_b = imag_a * cos_twist - real_a * sin_twist
    real_x = right_mul(real_b, cos_inner) + right_mul(imag_b, sin_inner)
    imag_x = right_mul(imag_b, cos_inner) - right_mul(real_b, sin_inner)
    return (real_x, imag_x)


def inverse_upper(real_x, imag_x, tables):
    cos_outer, sin_outer, cos_inner, sin_inner, cos_twist, sin_twist = tables
    real_c = right_mul(real_x, cos_inner) - right_mul(imag_x, sin_inner)
    imag_c = right_mul(imag_x, cos_inner) + right_mul(real_x, sin_inner)
    real_d = real_c * cos_twist - imag_c * sin_twist
    imag_d = imag_c * cos_twist + real_c * sin_twist
    middle = cos_outer.shape[0] // 2
    signal = left_mul(cos_outer[middle:], real_d) - left_mul(sin_outer[middle:], imag_d)
    return signal / float(cos_outer.shape[0] * lane_width)


def on_device(gate_in, key_in, value_in, kernel, skip_gain, out_weight):
    seg_index = lax.axis_index("seg")
    col_gate, col_key, col_value = (
        lax.all_to_all(gate_in, "seg", split_axis=0, concat_axis=1, tiled=True),
        lax.all_to_all(key_in, "seg", split_axis=0, concat_axis=1, tiled=True),
        lax.all_to_all(value_in, "seg", split_axis=0, concat_axis=1, tiled=True),
    )
    col_count, full_len = col_key.shape
    long_outer = 2 * full_len // lane_width
    long_tables = make_tables(long_outer)
    first = seg_index * col_count
    my_kernel = lax.dynamic_slice_in_dim(kernel, first, col_count, 0)
    my_skip = lax.dynamic_slice_in_dim(skip_gain, first, col_count, 0)
    col_mixed = col_key.astype(jnp.float32) * col_value.astype(jnp.float32)
    long_filter = jnp.concatenate(
        [jnp.zeros((col_count, full_len), jnp.float32), my_kernel], axis=1
    )
    filt_re, filt_im = forward(long_filter.reshape(col_count, long_outer, lane_width), long_tables)
    sig_re, sig_im = forward(col_mixed.reshape(col_count, long_outer // 2, lane_width), long_tables)
    prod_re = filt_re * sig_re - filt_im * sig_im
    prod_im = filt_re * sig_im + filt_im * sig_re
    col_conv = inverse_upper(prod_re, prod_im, long_tables).reshape(col_count, full_len)
    col_gated = (col_gate.astype(jnp.float32) * (col_conv + my_skip[:, None] * col_mixed)).astype(
        jnp.bfloat16
    )
    gated = lax.all_to_all(col_gated, "seg", split_axis=1, concat_axis=0, tiled=True)
    result = lax.psum_scatter(
        lax.dot_general(
            gated, out_weight, (((0,), (0,)), ((), ())), preferred_element_type=jnp.float32
        ),
        "ch",
        scatter_dimension=0,
        tiled=True,
    )
    return result.astype(jnp.bfloat16)


def solution(mesh):
    placed = (P("ch", "seg"), P("ch", "seg"), P("ch", "seg"), P("ch", None), P("ch"), P("ch", None))
    return jax.shard_map(
        on_device, mesh=mesh, in_specs=placed, out_specs=P(("seg", "ch"), None), check_vma=False
    )
```

profile of v0, /device:TPU:0, one launch (start us, length us, event | category | flops | bytes accessed | tf_op | source)
XLA Modules:
  0.0 486.7 jit_solution(11447293590223693794)
XLA Ops:
  6.5 6.5 %all-to-all-start.1 = ((bf16[4,48,4096]{2,1,0:T(8,128)(2,1)}), bf16[4,48,4096]{2,1,0:T(8,128)(2,1)}, u32[]{:S(2)}, u32[]{:S(2)}) async-start(bf16[4,48,4096]{2,1,0:T(8,128)(2,1)} %bitcast.134), calls=%async_computation.1 | async-start | bytes 3145728 | tf_op jit(solution)/shard_map/all_to_all | solution.py:64
  17.2 11.6 %fusion.44 = f32[48,128,256]{2,1,0:T(8,128)S(1)} fusion(f32[48,256,128]{2,1,0:T(8,128)S(1)} %bitcast.131), kind=kOutput, calls=%fused_computation.51 | convolution fusion | flops 4832755712 | bytes 12582912 | tf_op jit(solution)/shard_map/kn,cnm->ckm/dot_general | solution.py:30
  28.9 21.4 %fusion.46 = f32[48,128,256]{2,1,0:T(8,128)S(1)} fusion(f32[48,256,128]{2,1,0:T(8,128)S(1)} %bitcast.132), kind=kOutput, calls=%fused_computation.53 | convolution fusion | flops 4832755712 | bytes 12582912 | tf_op jit(solution)/shard_map/kn,cnm->ckm/dot_general | solution.py:30
  50.3 2.6 copy-done.3
  52.8 12.4 %fusion.23 = f32[48,256,128]{2,1,0:T(8,128)} fusion(f32[48,128,256]{2,1,0:T(8,128)S(1)} %fusion.46, f32[48,128,256]{2,1,0:T(8,128)S(1)} %fusion.44, f32[256,128]{0,1:T(8,128)S(1)} %get-tuple-element.7, f32[256,128]{0,1:T(8,128)S(1)} %get-tuple-element.8), kind=kOutput, calls=%fused_computation.37 | convolution fusion | flops 2422439936 | bytes 19136512 | tf_op jit(solution)/shard_map/ckn,nm->ckm/dot_general | solution.py:34
  65.3 5.1 %all-to-all-start.2 = ((bf16[4,48,4096]{2,1,0:T(8,128)(2,1)}), bf16[4,48,4096]{2,1,0:T(8,128)(2,1)}, u32[]{:S(2)}, u32[]{:S(2)}) async-start(bf16[4,48,4096]{2,1,0:T(8,128)(2,1)} %bitcast.135), calls=%async_computation.2 | async-start | bytes 3145728 | tf_op jit(solution)/shard_map/all_to_all | solution.py:65
  72.4 15.9 %fusion.25 = f32[48,256,128]{2,1,0:T(8,128)} fusion(f32[48,128,256]{2,1,0:T(8,128)} %copy-done.3, f32[48,128,256]{2,1,0:T(8,128)} %copy-done.2, f32[256,128]{0,1:T(8,128)S(1)} %get-tuple-element.7, f32[256,128]{0,1:T(8,128)S(1)} %get-tuple-element.8), kind=kOutput, calls=%fused_computation.38 | convolution fusion | flops 2422439936 | bytes 19136512 | tf_op jit(solution)/shard_map/ckn,nm->ckm/dot_general | solution.py:34
  88.3 12.9 %fusion.27 = f32[48,256,128]{2,1,0:T(8,128)} fusion(f32[48,128,256]{2,1,0:T(8,128)S(1)} %bitcast.128, f32[48,128,256]{2,1,0:T(8,128)S(1)} %bitcast.126, f32[256,128]{0,1:T(8,128)S(1)} %get-tuple-element.7, f32[256,128]{0,1:T(8,128)S(1)} %get-tuple-element.8), kind=kOutput, calls=%fused_computation.39 | convolution fusion | flops 2422439936 | bytes 19136512 | tf_op jit(solution)/shard_map/ckn,nm->ckm/dot_general | solution.py:34
  101.1 12.4 %fusion.29 = f32[48,256,128]{2,1,0:T(8,128)} fusion(f32[48,128,256]{2,1,0:T(8,128)S(1)} %bitcast.128, f32[48,128,256]{2,1,0:T(8,128)S(1)} %bitcast.126, f32[256,128]{0,1:T(8,128)S(1)} %get-tuple-element.7, f32[256,128]{0,1:T(8,128)S(1)} %get-tuple-element.8), kind=kOutput, calls=%fused_computation.40 | convolution fusion | flops 2422439936 | bytes 19136512 | tf_op jit(solution)/shard_map/ckn,nm->ckm/dot_general | solution.py:34
  113.6 5.1 %all-to-all-start = ((bf16[4,48,4096]{2,1,0:T(8,128)(2,1)}), bf16[4,48,4096]{2,1,0:T(8,128)(2,1)}, u32[]{:S(2)}, u32[]{:S(2)}) async-start(bf16[4,48,4096]{2,1,0:T(8,128)(2,1)} %bitcast.136), calls=%async_computation | async-start | bytes 3145728 | tf_op jit(solution)/shard_map/all_to_all | solution.py:63
  118.7 2.3 fusion.18
  121.0 3.7 copy.40
  124.7 5.4 %mul.450 = f32[48,128,128]{2,1,0:T(8,128)} reshape(f32[48,4,4096]{2,1,0:T(4,128)} %copy.40) | data formatting | bytes 6291456 | tf_op jit(solution)/shard_map/mul | solution.py:73
  130.1 7.4 %fusion.54 = f32[48,128,256]{2,1,0:T(8,128)S(1)} fusion(f32[48,128,128]{2,1,0:T(8,128)} %mul.450, f32[256,256]{1,0:T(8,128)S(1)} %fusion.58), kind=kOutput, calls=%fused_computation.67 | convolution fusion | flops 2415919104 | bytes 9568256 | tf_op jit(solution)/shard_map/kn,cnm->ckm/dot_general | solution.py:30
  137.6 5.4 %fusion.55 = f32[48,128,256]{2,1,0:T(8,128)S(1)} fusion(f32[48,128,128]{2,1,0:T(8,128)S(1)} %copy-done.5, f32[256,256]{1,0:T(8,128)S(1)} %fusion.59), kind=kOutput, calls=%fused_computation.69 | convolution fusion | flops 2415919104 | bytes 9568256 | tf_op jit(solution)/shard_map/kn,cnm->ckm/dot_general | solution.py:30
  143.0 12.7 %fusion.33 = f32[48,256,128]{2,1,0:T(8,128)} fusion(f32[48,128,256]{2,1,0:T(8,128)S(1)} %fusion.55, f32[48,128,256]{2,1,0:T(8,128)S(1)} %fusion.54, f32[256,128]{0,1:T(8,128)S(1)} %get-tuple-element.7, f32[256,128]{0,1:T(8,128)S(1)} %get-tuple-element.8), kind=kOutput, calls=%fused_computation.42 | convolution fusion | flops 2422439936 | bytes 19136512 | tf_op jit(solution)/shard_map/ckn,nm->ckm/dot_general | solution.py:34
  155.7 12.5 %fusion.37 = f32[48,256,128]{2,1,0:T(8,128)} fusion(f32[48,128,256]{2,1,0:T(8,128)S(1)} %fusion.55, f32[48,128,256]{2,1,0:T(8,128)S(1)} %fusion.54, f32[256,128]{0,1:T(8,128)S(1)} %get-tuple-element.7, f32[256,128]{0,1:T(8,128)S(1)} %get-tuple-element.8), kind=kOutput, calls=%fused_computation.44 | convolution fusion | flops 2422439936 | bytes 19136512 | tf_op jit(solution)/shard_map/ckn,nm->ckm/dot_general | solution.py:34
  168.2 12.9 %fusion.35 = f32[48,256,128]{2,1,0:T(8,128)} fusion(f32[48,128,256]{2,1,0:T(8,128)S(1)} %fusion.55, f32[48,128,256]{2,1,0:T(8,128)S(1)} %fusion.54, f32[256,128]{0,1:T(8,128)S(1)} %get-tuple-element.7, f32[256,128]{0,1:T(8,128)S(1)} %get-tuple-element.8), kind=kOutput, calls=%fused_computation.43 | convolution fusion | flops 2422439936 | bytes 19136512 | tf_op jit(solution)/shard_map/ckn,nm->ckm/dot_general | solution.py:34
  181.1 25.2 %multiply_subtract_fusion = (f32[48,256,128]{2,1,0:T(8,128)}, f32[48,256,128]{2,1,0:T(8,128)}) fusion(f32[48,256,128]{2,1,0:T(8,128)} %fusion.35, f32[48,256,128]{2,1,0:T(8,128)} %fusion.23, f32[48,256,128]{2,1,0:T(8,128)} %fusion.27, f32[48,256,128]{2,1,0:T(8,128)} %fusion.37, f32[48,256,128]{2,1,0:T(8,128)} %fusion.33, f32[48,256,128]{2,1,0:T(8,128)} %fusion.29, ...), kind=kOutput, calls=%fused_computation.21 | convolution fusion | flops 2438168576 | bytes 69468160 | tf_op jit(solution)/shard_map/ckn,nm->ckm/dot_general | solution.py:34
  206.4 9.4 %fusion.68 = f32[48,256,128]{1,2,0:T(8,128)S(1)} fusion(f32[48,256,128]{2,1,0:T(8,128)} %get-tuple-element.6), kind=kOutput, calls=%fused_computation.83 | convolution fusion | flops 2416148480 | bytes 12582912 | tf_op jit(solution)/shard_map/ckn,nm->ckm/dot_general | solution.py:34
  215.8 6.7 %fusion.74 = f32[48,256,128]{1,2,0:T(8,128)S(1)} fusion(f32[48,256,128]{2,1,0:T(8,128)S(1)} %copy-done.4), kind=kOutput, calls=%fused_computation.89 | convolution fusion | flops 2416148480 | bytes 12582912 | tf_op jit(solution)/shard_map/ckn,nm->ckm/dot_general | solution.py:34
  222.5 6.9 %fusion.66 = f32[48,256,128]{1,2,0:T(8,128)S(1)} fusion(f32[48,256,128]{2,1,0:T(8,128)S(1)} %bitcast.130), kind=kOutput, calls=%fused_computation.81 | convolution fusion | flops 2416148480 | bytes 12582912 | tf_op jit(solution)/shard_map/ckn,nm->ckm/dot_general | solution.py:34
  229.4 8.0 %fusion.76 = f32[48,256,128]{1,2,0:T(8,128)} fusion(f32[48,256,128]{2,1,0:T(8,128)S(1)} %bitcast.130), kind=kOutput, calls=%fused_computation.91 | convolution fusion | flops 2416148480 | bytes 12582912 | tf_op jit(solution)/shard_map/ckn,nm->ckm/dot_general | solution.py:34
  237.4 9.0 %fusion.4 = f32[48,128,128]{2,1,0:T(8,128)} fusion(f32[256,128]{0,1:T(8,128)S(1)} %get-tuple-element.7, f32[256,128]{0,1:T(8,128)S(1)} %get-tuple-element.8, f32[48,256,128]{1,2,0:T(8,128)S(1)} %fusion.74, f32[48,256,128]{1,2,0:T(8,128)S(1)} %fusion.66, f32[48,256,128]{1,2,0:T(8,128)} %fusion.76, f32[48,256,128]{1,2,0:T(8,128)S(1)} %fusion.68, ...), kind=kOutput, calls=%fused_computation.12 | convolution fusion | flops 2423783424 | bytes 28704768 | tf_op jit(solution)/shard_map/kn,cnm->ckm/dot_general | solution.py:30
  246.4 9.5 %multiply_bitcast_fusion = f32[48,128,128]{1,2,0:T(8,128)} fusion(f32[48,128,128]{2,1,0:T(8,128)} %fusion.4, f32[256,128]{0,1:T(8,128)S(1)} %get-tuple-element.7, f32[256,128]{0,1:T(8,128)S(1)} %get-tuple-element.8, f32[48,256,128]{1,2,0:T(8,128)S(1)} %fusion.74, f32[48,256,128]{1,2,0:T(8,128)S(1)} %fusion.66, f32[48,256,128]{1,2,0:T(8,128)} %fusion.76, ...), kind=kOutput, calls=%fused_computation.26 | convolution fusion | flops 2425356288 | bytes 31850496 | tf_op jit(solution)/shard_map/kn,cnm->ckm/dot_general | solution.py:30
  255.9 3.6 copy.53
  259.5 5.1 %reshape.68 = f32[48,4,4096]{2,1,0:T(4,128)} reshape(f32[48,128,128]{2,1,0:T(8,128)} %copy.53) | data formatting | bytes 6291456 | tf_op jit(solution)/shard_map/reshape | solution.py:81
  264.6 5.7 %fusion.13 = bf16[48,4,4096]{2,0,1:T(8,128)(2,1)S(1)} fusion(f32[48,4,4096]{2,1,0:T(4,128)} %reshape.68, bf16[4,48,4096]{2,1,0:T(8,128)(2,1)} %all-to-all-done, bf16[4,48,4096]{2,1,0:T(8,128)(2,1)} %all-to-all-done.2, bf16[4,48,4096]{2,1,0:T(8,128)(2,1)} %all-to-all-done.1, f32[48]{0:T(128)S(1)} %dynamic_slice.7), kind=kLoop, calls=%fused_computation.25 | loop fusion | flops 6291456 | bytes 9437376 | tf_op jit(solution)/shard_map/convert_element_type | solution.py:82
  270.3 40.2 %all_to_all.55 = bf16[48,4,4096]{2,0,1:T(8,128)(2,1)S(1)} all-to-all(bf16[48,4,4096]{2,0,1:T(8,128)(2,1)S(1)} %fusion.13), channel_id=1, replica_groups=mesh['seg'=4,'ch'=8] {'seg'}, dimensions={1} | all-to-all | bytes 3145728 | tf_op jit(solution)/shard_map/all_to_all | solution.py:85
  310.5 10.1 %fusion.157 = f32[4096,1536]{1,0:T(8,128)} fusion(bf16[192,4096]{1,0:T(8,128)(2,1)S(1)} %bitcast.133, bf16[192,1536]{1,0:T(8,128)(2,1)S(1)} %copy-done), kind=kOutput, calls=%fused_computation.161 | convolution fusion | flops 2415919104 | bytes 27328512 | tf_op jit(solution)/shard_map/dot_general | solution.py:87
  320.7 155.6 %reduce-scatter.2.cloned.1.call-done = f32[512,1536]{1,0:T(8,128)} async-done(((f32[4096,1536]{1,0:T(8,128)}), f32[512,1536]{1,0:T(8,128)}) %reduce-scatter.2.cloned.1.call-update) | async-done | bytes 3145744 | tf_op jit(solution)/shard_map/reduce_scatter | solution.py:86
  476.2 3.2 convert_element_type.108
  (40 shorter events, 6.2 us)
Async XLA Ops:
  6.5 304.0 %copy-start = (bf16[192,1536]{1,0:T(8,128)(2,1)S(1)}, bf16[192,1536]{1,0:T(8,128)(2,1)}, u32[]{:S(2)}) copy-start(bf16[192,1536]{1,0:T(8,128)(2,1)} %param.11) | copy-start | bytes 1769476
  6.5 58.7 %all-to-all-start.1 = ((bf16[4,48,4096]{2,1,0:T(8,128)(2,1)}), bf16[4,48,4096]{2,1,0:T(8,128)(2,1)}, u32[]{:S(2)}, u32[]{:S(2)}) async-start(bf16[4,48,4096]{2,1,0:T(8,128)(2,1)} %bitcast.134), calls=%async_computation.1 | async-start | bytes 3145728 | tf_op jit(solution)/shard_map/all_to_all | solution.py:64
  15.5 1.1 copy-start.6
  28.8 21.4 %copy-start.2 = (f32[48,128,256]{2,1,0:T(8,128)}, f32[48,128,256]{2,1,0:T(8,128)S(1)}, u32[]{:S(2)}) copy-start(f32[48,128,256]{2,1,0:T(8,128)S(1)} %fusion.44) | copy-start | bytes 18874372
  50.3 2.6 copy-start.3
  65.3 48.3 %all-to-all-start.2 = ((bf16[4,48,4096]{2,1,0:T(8,128)(2,1)}), bf16[4,48,4096]{2,1,0:T(8,128)(2,1)}, u32[]{:S(2)}, u32[]{:S(2)}) async-start(bf16[4,48,4096]{2,1,0:T(8,128)(2,1)} %bitcast.135), calls=%async_computation.2 | async-start | bytes 3145728 | tf_op jit(solution)/shard_map/all_to_all | solution.py:65
  71.3 16.9 %slice-start = ((s8[6291456]{0:T(1024)(128)(4,1)}), s8[4194304]{0:T(1024)(128)(4,1)S(1)}, s32[]{:S(2)}) async-start(s8[6291456]{0:T(1024)(128)(4,1)} %bitcast.125), calls=%async_computation.6 | async-start | bytes 8388608
  71.4 16.9 %slice-start.2 = ((s8[6291456]{0:T(1024)(128)(4,1)}), s8[4194304]{0:T(1024)(128)(4,1)S(1)}, s32[]{:S(2)}) async-start(s8[6291456]{0:T(1024)(128)(4,1)} %bitcast.127), calls=%async_computation.8 | async-start | bytes 8388608
  72.3 15.9 %slice-start.1 = ((s8[6291456]{0:T(1024)(128)(4,1)}), s8[2097152]{0:T(1024)(128)(4,1)S(1)}, s32[]{:S(2)}) async-start(s8[6291456]{0:T(1024)(128)(4,1)} %bitcast.125), calls=%async_computation.7 | async-start | bytes 4194304
  72.3 15.9 %slice-start.3 = ((s8[6291456]{0:T(1024)(128)(4,1)}), s8[2097152]{0:T(1024)(128)(4,1)S(1)}, s32[]{:S(2)}) async-start(s8[6291456]{0:T(1024)(128)(4,1)} %bitcast.127), calls=%async_computation.9 | async-start | bytes 4194304
  113.6 151.1 %all-to-all-start = ((bf16[4,48,4096]{2,1,0:T(8,128)(2,1)}), bf16[4,48,4096]{2,1,0:T(8,128)(2,1)}, u32[]{:S(2)}, u32[]{:S(2)}) async-start(bf16[4,48,4096]{2,1,0:T(8,128)(2,1)} %bitcast.136), calls=%async_computation | async-start | bytes 3145728 | tf_op jit(solution)/shard_map/all_to_all | solution.py:63
  118.7 357.6 %reduce-scatter.2.cloned.1.call-start = ((), (), s32[]{:S(2)}) async-start(), calls=%async_computation.5 | async-start | bytes 28311552 | tf_op jit(solution)/shard_map/reduce_scatter | solution.py:86
  130.1 7.5 %copy-start.5 = (f32[48,128,128]{2,1,0:T(8,128)S(1)}, f32[48,128,128]{2,1,0:T(8,128)}, u32[]{:S(2)}) copy-start(f32[48,128,128]{2,1,0:T(8,128)} %mul.450) | copy-start | bytes 9437188
  143.0 25.2 %copy-start.1 = (f32[48,128,256]{2,1,0:T(8,128)}, f32[48,128,256]{2,1,0:T(8,128)S(1)}, u32[]{:S(2)}) copy-start(f32[48,128,256]{2,1,0:T(8,128)S(1)} %fusion.55) | copy-start | bytes 18874372
  206.4 9.4 %copy-start.4 = (f32[48,256,128]{2,1,0:T(8,128)S(1)}, f32[48,256,128]{2,1,0:T(8,128)}, u32[]{:S(2)}) copy-start(f32[48,256,128]{2,1,0:T(8,128)} %get-tuple-element.6) | copy-start | bytes 18874372
  206.4 16.1 %slice-start.4 = ((s8[6291456]{0:T(1024)(128)(4,1)}), s8[4194304]{0:T(1024)(128)(4,1)S(1)}, s32[]{:S(2)}) async-start(s8[6291456]{0:T(1024)(128)(4,1)} %bitcast.129), calls=%async_computation.10 | async-start | bytes 8388608
  215.8 6.7 %slice-start.5 = ((s8[6291456]{0:T(1024)(128)(4,1)}), s8[2097152]{0:T(1024)(128)(4,1)S(1)}, s32[]{:S(2)}) async-start(s8[6291456]{0:T(1024)(128)(4,1)} %bitcast.129), calls=%async_computation.11 | async-start | bytes 4194304
Sparse Core Ops, SparseCore 0:
  320.8 155.3 reduce-scatter.1
where the time goes:
time: 496 us; the launch traced here: 487 us
  matrix products  222 us (45%)
  waiting for transfers between devices  156 us (31%)
  blocking collectives  40.2 us (8%)
  local copies, waits for them, and re-layouts  24.1 us (5%)
  starting transfers between devices  16.7 us (3%)
  between operations  14.1 us (3%)
  other arithmetic  13.6 us (3%)
    reduce_scatter x1, waiting for transfers between devices, on_device(): lax.psum_scatter(lax.dot_general(gated, out_weight, (((0,), (0,)), ((), (...  156 us
    dot_general x12, matrix products, right_mul(): return jnp.einsum('ckn,nm->ckm', stack, matrix, precision=highest)  148 us
    dot_general x6, matrix products, left_mul(): return jnp.einsum('kn,cnm->ckm', matrix, stack, precision=highest)  64.4 us
    all_to_all x1, blocking collectives, on_device(): lax.all_to_all(col_gated, 'seg', split_axis=1, concat_axis=0, tiled=True)  40.2 us
    dot_general x1, matrix products, on_device(): lax.dot_general(gated, out_weight, (((0,), (0,)), ((), ())), preferred_el...  10.1 us
  transfers between devices with their start and end apart: 4, of which 1 were waited for; matrix products, arithmetic and copies ran while one was open for 49% of the time, Pallas kernels for 0%

commit v1 on v0

v1 whole, which is shorter than its diff:
```python
import functools
import math

import jax
import jax.numpy as jnp
from jax import lax
from jax.experimental import pallas as pl
from jax.experimental.pallas import tpu as pltpu
from jax.sharding import PartitionSpec as P

lane_width = 128
bf16 = jnp.bfloat16
f32 = jnp.float32


def angles(rows, cols, period):
    product = rows[:, None] * cols[None, :] % (4 * period)
    theta = product.astype(f32) * (2.0 * math.pi / (4 * period))
    return jnp.cos(theta), jnp.sin(theta)


def make_tables(outer):
    quarter = 4 * jnp.arange(outer, dtype=jnp.int32) + 1
    row = jnp.arange(outer, dtype=jnp.int32)
    lane = jnp.arange(lane_width, dtype=jnp.int32)
    cos_o, sin_o = angles(quarter, row, outer)
    cos_t, sin_t = angles(quarter, lane, outer * lane_width)
    cos_i, sin_i = angles(4 * lane, lane, lane_width)
    first = jnp.concatenate([cos_o, -sin_o], axis=0).astype(bf16)
    last = (jnp.concatenate([cos_o.T, -sin_o.T], axis=1) / (outer * lane_width)).astype(bf16)
    inner = jnp.block([[cos_i, -sin_i], [sin_i, cos_i]]).astype(bf16)
    inner_back = jnp.block([[cos_i, sin_i], [-sin_i, cos_i]]).astype(bf16)
    return first, last, inner, inner_back, cos_t, sin_t


def forward(signal, first, inner, cos_t, sin_t):
    outer = cos_t.shape[0]
    rows = []
    for at in range(0, len(signal), 2):
        pair = signal[at : at + 2]
        wide = jnp.dot(first, jnp.concatenate(pair, axis=1), preferred_element_type=f32)
        for i in range(len(pair)):
            part = wide[:, i * lane_width : (i + 1) * lane_width]
            real, imag = part[:outer], part[outer:]
            rows.append(
                jnp.concatenate(
                    [
                        (real * cos_t + imag * sin_t).astype(bf16),
                        (imag * cos_t - real * sin_t).astype(bf16),
                    ],
                    axis=1,
                )
            )
    return jnp.dot(jnp.concatenate(rows, axis=0), inner, preferred_element_type=f32)


def filter_kernel(first, inner, cos_t, sin_t, taps, spectrum):
    count, outer = taps.shape[0], taps.shape[1]
    signal = [taps[i].astype(bf16) for i in range(count)]
    out = forward(signal, first[...], inner[...], cos_t[...], sin_t[...])
    spectrum[...] = out.astype(bf16).reshape(count, outer, 2 * lane_width)


def conv_kernel(first, last, inner, inner_back, cos_t, sin_t, mixed, spectrum, conv):
    count, outer = mixed.shape[0], mixed.shape[1]
    cos, sin = cos_t[...], sin_t[...]
    sig = forward([mixed[i] for i in range(count)], first[...], inner[...], cos, sin)
    filt = spectrum[...].reshape(count * outer, 2 * lane_width).astype(f32)
    sig_re, sig_im = sig[:, :lane_width], sig[:, lane_width:]
    filt_re, filt_im = filt[:, :lane_width], filt[:, lane_width:]
    prod = jnp.concatenate(
        [
            (filt_re * sig_re - filt_im * sig_im).astype(bf16),
            (filt_re * sig_im + filt_im * sig_re).astype(bf16),
        ],
        axis=1,
    )
    back = jnp.dot(prod, inner_back[...], preferred_element_type=f32)
    for at in range(0, count, 2):
        cols = []
        for i in range(at, min(at + 2, count)):
            rows = back[i * outer : (i + 1) * outer]
            real, imag = rows[:, :lane_width], rows[:, lane_width:]
            cols.append(
                jnp.concatenate(
                    [
                        (real * cos - imag * sin).astype(bf16),
                        (imag * cos + real * sin).astype(bf16),
                    ],
                    axis=0,
                )
            )
        wide = jnp.dot(last[...], jnp.concatenate(cols, axis=1), preferred_element_type=f32)
        for i in range(len(cols)):
            conv[at + i] = wide[:, i * lane_width : (i + 1) * lane_width].astype(bf16)


def whole(array):
    return pl.BlockSpec(array.shape, lambda i: (0,) * array.ndim)


def block_of(count):
    return max(b for b in range(1, 9) if count % b == 0)


def transform_filter(tables, taps):
    first, last, inner, inner_back, cos_t, sin_t = tables
    count, outer, lanes = taps.shape
    block = block_of(count)
    fixed = (first, inner, cos_t, sin_t)
    return pl.pallas_call(
        filter_kernel,
        grid=(count // block,),
        in_specs=[whole(a) for a in fixed] + [pl.BlockSpec((block, outer, lanes), lambda i: (i, 0, 0))],
        out_specs=pl.BlockSpec((block, outer, 2 * lanes), lambda i: (i, 0, 0)),
        out_shape=jax.ShapeDtypeStruct((count, outer, 2 * lanes), bf16),
        cost_estimate=pl.CostEstimate(
            flops=count * outer * lanes * 1536, bytes_accessed=count * outer * lanes * 8, transcendentals=0
        ),
        name="filter_transform",
    )(*fixed, taps)


def convolve(tables, mixed, spectrum):
    count, outer, lanes = mixed.shape
    block = block_of(count)
    return pl.pallas_call(
        conv_kernel,
        grid=(count // block,),
        in_specs=[whole(a) for a in tables]
        + [
            pl.BlockSpec((block, outer, lanes), lambda i: (i, 0, 0)),
            pl.BlockSpec((block, outer, 2 * lanes), lambda i: (i, 0, 0)),
        ],
        out_specs=pl.BlockSpec((block, outer, lanes), lambda i: (i, 0, 0)),
        out_shape=jax.ShapeDtypeStruct((count, outer, lanes), bf16),
        cost_estimate=pl.CostEstimate(
            flops=count * outer * lanes * 3072, bytes_accessed=count * outer * lanes * 8, transcendentals=0
        ),
        name="convolve",
    )(*tables, mixed, spectrum)


def on_device(gate_in, key_in, value_in, kernel, skip_gain, out_weight):
    seg_count = lax.axis_size("seg")
    seg_index = lax.axis_index("seg")
    channels, tokens = key_in.shape
    full_len = kernel.shape[1]
    outer = full_len // lane_width
    tables = make_tables(outer)
    col_count = channels // seg_count
    mixed = key_in.astype(f32) * value_in.astype(f32)
    mixed_sent = mixed.astype(bf16).reshape(channels, tokens // lane_width, lane_width)
    col_mixed = lax.all_to_all(mixed_sent, "seg", split_axis=0, concat_axis=1, tiled=True)
    taps = lax.dynamic_slice_in_dim(kernel, seg_index * col_count, col_count, 0)
    spectrum = transform_filter(tables, taps.astype(bf16).reshape(col_count, outer, lane_width))
    col_conv = convolve(tables, col_mixed, spectrum)
    conv = lax.all_to_all(col_conv, "seg", split_axis=1, concat_axis=0, tiled=True)
    conv = conv.reshape(channels, tokens).astype(f32)
    gated = (gate_in.astype(f32) * (conv + skip_gain[:, None] * mixed)).astype(bf16)
    mine = lax.all_to_all(gated, "ch", split_axis=1, concat_axis=0, tiled=True)
    weight = lax.all_gather(out_weight, "ch", axis=0, tiled=True)
    result = lax.dot_general(
        mine, weight, (((0,), (0,)), ((), ())), preferred_element_type=f32
    )
    return result.astype(bf16)


def solution(mesh):
    placed = (P("ch", "seg"), P("ch", "seg"), P("ch", "seg"), P("ch", None), P("ch"), P("ch", None))
    return jax.shard_map(
        on_device, mesh=mesh, in_specs=placed, out_specs=P(("seg", "ch"), None), check_vma=False
    )
```

time: 496 us -> 150 us (0.30); the launches traced: 487 us -> 149 us
  matrix products: 222 us -> 6.05 us
  waiting for transfers between devices: 156 us -> 23.5 us
  blocking collectives: 40.2 us -> 63.4 us
  Pallas kernels: 0 us -> 14.6 us
  local copies, waits for them, and re-layouts: 24.1 us -> 12 us
  starting transfers between devices: 16.7 us -> 6.35 us
    dot_general x19 -> x1, matrix products: 222 us -> 6.05 us  [on_device(): lax.dot_general(mine, weight, (((0,), (0,)), ((), ())), preferred_element...]
    reduce_scatter x1 -> x0, waiting for transfers between devices: 156 us -> none  [on_device(): lax.psum_scatter(lax.dot_general(gated, out_weight, (((0,), (0,)), ((), (...]
    all_to_all x1 -> x2, blocking collectives: 40.2 us -> 63.4 us  [the longest x1 39 us: on_device(): lax.all_to_all(col_conv, 'seg', split_axis=1, concat_axis=0, tiled=True)]
    all_to_all x3 -> x1, waiting for transfers between devices: 0.01 us -> 22.8 us  [on_device(): lax.all_to_all(mixed_sent, 'seg', split_axis=0, concat_axis=1, tiled=True)]
    pallas_call x0 -> x2, Pallas kernels: none -> 14.6 us  [the longest x1 8.18 us: convolve(): pl.pallas_call(conv_kernel, grid=(count // block,), in_specs=[whole(a) fo...]
    all_to_all x3 -> x1, starting transfers between devices: 16.7 us -> 6.35 us  [on_device(): lax.all_to_all(mixed_sent, 'seg', split_axis=0, concat_axis=1, tiled=True)]
    mul x2 -> x0, local copies, waits for them, and re-layouts: 9.1 us -> none  [on_device(): col_mixed = col_key.astype(jnp.float32) * col_value.astype(jnp.float32)]
    reshape x1 -> x0, local copies, waits for them, and re-layouts: 5.13 us -> none  [on_device(): inverse_upper(prod_re, prod_im, long_tables).reshape(col_count, full_len)]
  transfers between devices with their start and end apart: 4 -> 2, of which waited for: 1 -> 1; matrix products, arithmetic and copies ran while one was open for 49% -> 14% of each run, Pallas kernels for 0% -> 10%
where the time goes in v1:
time: 150 us; the launch traced here: 149 us
  blocking collectives  63.4 us (42%)
  waiting for transfers between devices  23.5 us (16%)
  Pallas kernels  14.6 us (10%)
  between operations  13.5 us (9%)
  local copies, waits for them, and re-layouts  12 us (8%)
  other arithmetic  9.75 us (6%)
  starting transfers between devices  6.35 us (4%)
  matrix products  6.05 us (4%)
    all_to_all x1, blocking collectives, on_device(): lax.all_to_all(col_conv, 'seg', split_axis=1, concat_axis=0, tiled=True)  39 us
    all_to_all x1, blocking collectives, on_device(): mine = lax.all_to_all(gated, 'ch', split_axis=1, concat_axis=0, tiled=True)  24.5 us
    all_to_all x1, waiting for transfers between devices, on_device(): lax.all_to_all(mixed_sent, 'seg', split_axis=0, concat_axis=1, tiled=True)  22.8 us
    pallas_call x1, Pallas kernels, convolve(): pl.pallas_call(conv_kernel, grid=(count // block,), in_specs=[whole(a) fo...  8.18 us
    unnamed x11, local copies, waits for them, and re-layouts  6.84 us
    pallas_call x1, Pallas kernels, transform_filter(): pl.pallas_call(filter_kernel, grid=(count // block,), in_specs=[whole(a)...  6.41 us
    all_to_all x1, starting transfers between devices, on_device(): lax.all_to_all(mixed_sent, 'seg', split_axis=0, concat_axis=1, tiled=True)  6.35 us
    dot_general x1, matrix products, on_device(): lax.dot_general(mine, weight, (((0,), (0,)), ((), ())), preferred_element...  6.05 us
  transfers between devices with their start and end apart: 2, of which 1 were waited for; matrix products, arithmetic and copies ran while one was open for 14% of the time, Pallas kernels for 10%

profile of v1, /device:TPU:0, one launch (start us, length us, event | category | flops | bytes accessed | tf_op | source)
XLA Modules:
  0.0 149.1 jit_solution(3750254413019143323)
XLA Ops:
  6.5 0.0 all-gather.2.cloned.1.call-start
  6.5 0.7 all-gather.2.cloned.1.call-update
  7.3 2.4 %fusion.3 = bf16[24,8,32,128]{3,1,2,0:T(8,128)(2,1)S(1)} fusion(bf16[192,4096]{1,0:T(8,128)(2,1)} %param.8, bf16[192,4096]{1,0:T(8,128)(2,1)} %param.7), kind=kLoop, calls=%fused_computation.8 | loop fusion | flops 3145728 | bytes 4718592
  9.6 1.5 %copy.18 = bf16[24,8,32,128]{3,2,1,0:T(8,128)(2,1)} copy(bf16[24,8,32,128]{3,1,2,0:T(8,128)(2,1)S(1)} %fusion.3) | data formatting | bytes 3145728
  11.1 6.3 %all-to-all-start = ((bf16[192,32,128]{2,1,0:T(8,128)(2,1)}), bf16[192,32,128]{2,1,0:T(8,128)(2,1)S(1)}, u32[]{:S(2)}, u32[]{:S(2)}) async-start(bf16[192,32,128]{2,1,0:T(8,128)(2,1)} %bitcast.13), calls=%async_computation | async-start | bytes 3145728 | tf_op jit(solution)/shard_map/all_to_all | solution.py:154
  17.5 2.3 %fusion.4 = bf16[6,8,128,128]{3,1,2,0:T(8,128)(2,1)S(1)} fusion(f32[192,16384]{1,0:T(8,128)} %param.9, s32[]{:T(128)S(6)} %select_n.50), kind=kLoop, calls=%fused_computation.9 | loop fusion | bytes 3145732
  19.8 1.7 %copy.19 = bf16[6,8,128,128]{3,2,1,0:T(8,128)(2,1)} copy(bf16[6,8,128,128]{3,1,2,0:T(8,128)(2,1)S(1)} %fusion.4) | data formatting | bytes 3145728
  21.5 1.5 fusion.34
  22.9 0.6 pad_maximum_fusion.4.first
  23.5 0.3 negate_convert_fusion
  23.9 0.7 fusion.6
  24.6 6.4 %filter_transform.1.spectrum = bf16[48,128,256]{2,1,0:T(8,128)(2,1)} custom-call(bf16[256,128]{1,0:T(8,128)(2,1)} %pad_maximum_fusion.4.first, bf16[256,256]{1,0:T(8,128)(2,1)} %get-tuple-element.6.inner, f32[128,128]{1,0:T(8,128)} %get-tuple-element.12.cos_t, f32[128,128]{1,0:T(8,128)} %get-tuple-element.7.sin_t, bf16[48,128,128]{2,1,0:T(8,128)(2,1)} %bitcast.33), custom_call_target="tpu_custom_call" | custom-call | flops 1207959552 | bytes 6291456 | tf_op jit(solution)/shard_map/filter_transform/pallas_call | solution.py:111
  31.0 0.6 fusion.7.last
  31.7 22.8 %all-to-all-done = bf16[192,32,128]{2,1,0:T(8,128)(2,1)S(1)} async-done(((bf16[192,32,128]{2,1,0:T(8,128)(2,1)}), bf16[192,32,128]{2,1,0:T(8,128)(2,1)S(1)}, u32[]{:S(2)}, u32[]{:S(2)}) %all-to-all-start) | async-done | bytes 1572896 | tf_op jit(solution)/shard_map/all_to_all | solution.py:154
  54.4 1.6 %copy.13 = bf16[48,4,32,128]{3,2,1,0:T(8,128)(2,1)} copy(bf16[48,4,32,128]{3,2,0,1:T(8,128)(2,1)S(1)} %bitcast.32) | data formatting | bytes 3145728 | tf_op jit(solution)/shard_map/all_to_all | solution.py:154
  56.1 8.2 %convolve.1 = bf16[48,128,128]{2,1,0:T(8,128)(2,1)} custom-call(bf16[256,128]{1,0:T(8,128)(2,1)} %pad_maximum_fusion.4.first, bf16[128,256]{1,0:T(8,128)(2,1)} %fusion.7.last, bf16[256,256]{1,0:T(8,128)(2,1)} %get-tuple-element.6.inner, bf16[256,256]{1,0:T(8,128)(2,1)} %get-tuple-element.5.inner_back, f32[128,128]{1,0:T(8,128)} %get-tuple-element.12.cos_t, ...), custom_call_target="tpu_custom_call" | custom-call | flops 2415919104 | bytes 6291456 | tf_op jit(solution)/shard_map/convolve/pallas_call | solution.py:127
  64.2 2.4 %copy.14 = bf16[48,128,128]{2,0,1:T(8,128)(2,1)S(1)} copy(bf16[48,128,128]{2,1,0:T(8,128)(2,1)} %convolve.1) | data formatting | bytes 3145728 | tf_op jit(solution)/shard_map/convolve/pallas_call | solution.py:127
  66.7 39.0 %all_to_all.46 = bf16[48,128,128]{2,0,1:T(8,128)(2,1)S(1)} all-to-all(bf16[48,128,128]{2,0,1:T(8,128)(2,1)S(1)} %copy.14), channel_id=1, replica_groups=mesh['seg'=4,'ch'=8] {'seg'}, dimensions={1} | all-to-all | bytes 3145728 | tf_op jit(solution)/shard_map/all_to_all | solution.py:158
  105.6 0.3 convert_bitcast_fusion
  105.9 0.0 copy-start
  105.9 0.0 copy-start.1
  105.9 0.0 copy-start.2
  105.9 0.0 copy-start.3
  106.0 1.0 copy.15
  106.9 0.4 copy-done
  107.3 0.5 copy-done.1
  107.8 0.5 copy-done.2
  108.3 0.0 copy-done.3
  108.3 3.4 %fusion.1 = bf16[192,4096]{1,0:T(8,128)(2,1)S(1)} fusion(f32[24,8,32,128]{3,2,1,0:T(8,128)S(1)} %bitcast.31, bf16[192,4096]{1,0:T(8,128)(2,1)S(1)} %copy-done.2, bf16[192,4096]{1,0:T(8,128)(2,1)S(1)} %copy-done, bf16[192,4096]{1,0:T(8,128)(2,1)S(1)} %copy-done.1, f32[192]{0:T(256)S(1)} %copy-done.3), kind=kLoop, calls=%fused_computation.2 | loop fusion | flops 6291456 | bytes 9437952 | tf_op jit(solution)/shard_map/convert_element_type | solution.py:160
  111.6 0.1 copy.23
  111.8 24.5 %all_to_all.47 = bf16[192,8,512]{2,0,1:T(8,128)(2,1)S(1)} all-to-all(bf16[192,8,512]{2,0,1:T(8,128)(2,1)S(1)} %bitcast.35), channel_id=1, replica_groups=mesh['seg'=4,'ch'=8] {'ch'}, dimensions={1} | all-to-all | bytes 3145728 | tf_op jit(solution)/shard_map/all_to_all | solution.py:161
  136.2 6.1 %convolution_convert_fusion = bf16[512,1536]{1,0:T(8,128)(2,1)} fusion(bf16[1536,512]{1,0:T(8,128)(2,1)S(1)} %bitcast.38, bf16[1536,1536]{1,0:T(8,128)(2,1)} %all-gather.2.cloned.1.call-done), kind=kOutput, calls=%fused_computation.6 | convolution fusion | flops 2416705536 | bytes 7864320 | tf_op jit(solution)/shard_map/dot_general | solution.py:163
  (3 shorter events, 0.0 us)
Async XLA Ops:
  6.5 129.7 %all-gather.2.cloned.1.call-start = ((), (), s32[]{:S(2)}) async-start(), calls=%async_computation.3 | async-start | bytes 5308416 | tf_op jit(solution)/shard_map/all_gather | solution.py:162
  11.1 43.3 %all-to-all-start = ((bf16[192,32,128]{2,1,0:T(8,128)(2,1)}), bf16[192,32,128]{2,1,0:T(8,128)(2,1)S(1)}, u32[]{:S(2)}, u32[]{:S(2)}) async-start(bf16[192,32,128]{2,1,0:T(8,128)(2,1)} %bitcast.13), calls=%async_computation | async-start | bytes 3145728 | tf_op jit(solution)/shard_map/all_to_all | solution.py:154
  105.9 1.4 copy-start
  105.9 1.9 %copy-start.1 = (bf16[192,4096]{1,0:T(8,128)(2,1)S(1)}, bf16[192,4096]{1,0:T(8,128)(2,1)}, u32[]{:S(2)}) copy-start(bf16[192,4096]{1,0:T(8,128)(2,1)} %param.7) | copy-start | bytes 4718596
  105.9 2.3 %copy-start.2 = (bf16[192,4096]{1,0:T(8,128)(2,1)S(1)}, bf16[192,4096]{1,0:T(8,128)(2,1)}, u32[]{:S(2)}) copy-start(bf16[192,4096]{1,0:T(8,128)(2,1)} %param.6) | copy-start | bytes 4718596
  105.9 2.3 %copy-start.3 = (f32[192]{0:T(256)S(1)}, f32[192]{0:T(256)}, u32[]{:S(2)}) copy-start(f32[192]{0:T(256)} %param.10) | copy-start | bytes 2308
Sparse Core Ops, SparseCore 0:
  9.2 41.5 all-gather.1

commit v2 on v1

--- a/solution.py
+++ b/solution.py
@@ -61,11 +61,11 @@
     spectrum[...] = out.astype(bf16).reshape(count, outer, 2 * lane_width)
 
 
-def conv_kernel(first, last, inner, inner_back, cos_t, sin_t, mixed, spectrum, conv):
-    count, outer = mixed.shape[0], mixed.shape[1]
-    cos, sin = cos_t[...], sin_t[...]
-    sig = forward([mixed[i] for i in range(count)], first[...], inner[...], cos, sin)
-    filt = spectrum[...].reshape(count * outer, 2 * lane_width).astype(f32)
+def convolve_block(tables, signal, filt):
+    first, last, inner, inner_back, cos, sin = tables
+    outer = cos.shape[0]
+    sig = forward(signal, first, inner, cos, sin)
+    filt = filt.astype(f32)
     sig_re, sig_im = sig[:, :lane_width], sig[:, lane_width:]
     filt_re, filt_im = filt[:, :lane_width], filt[:, lane_width:]
     prod = jnp.concatenate(
@@ -75,10 +75,11 @@
         ],
         axis=1,
     )
-    back = jnp.dot(prod, inner_back[...], preferred_element_type=f32)
-    for at in range(0, count, 2):
+    back = jnp.dot(prod, inner_back, preferred_element_type=f32)
+    parts = []
+    for at in range(0, len(signal), 2):
         cols = []
-        for i in range(at, min(at + 2, count)):
+        for i in range(at, min(at + 2, len(signal))):
             rows = back[i * outer : (i + 1) * outer]
             real, imag = rows[:, :lane_width], rows[:, lane_width:]
             cols.append(
@@ -90,9 +91,19 @@
                     axis=0,
                 )
             )
-        wide = jnp.dot(last[...], jnp.concatenate(cols, axis=1), preferred_element_type=f32)
+        wide = jnp.dot(last, jnp.concatenate(cols, axis=1), preferred_element_type=f32)
         for i in range(len(cols)):
-            conv[at + i] = wide[:, i * lane_width : (i + 1) * lane_width].astype(bf16)
+            parts.append(wide[:, i * lane_width : (i + 1) * lane_width].astype(bf16))
+    return parts
+
+
+def conv_kernel(first, last, inner, inner_back, cos_t, sin_t, mixed, spectrum, conv):
+    count, outer = mixed.shape[0], mixed.shape[1]
+    tables = (first[...], last[...], inner[...], inner_back[...], cos_t[...], sin_t[...])
+    filt = spectrum[...].reshape(count * outer, 2 * lane_width)
+    parts = convolve_block(tables, [mixed[i] for i in range(count)], filt)
+    for i in range(count):
+        conv[i] = parts[i]
 
 
 def whole(array):
@@ -141,6 +152,227 @@
     )(*tables, mixed, spectrum)
 
 
+MESH = pl.DeviceIdType.MESH
+
+
+def layer_kernel(
+    first, last, inner, inner_back, cos_t, sin_t, key, value, gate, skip, kernel, weight,
+    gathered, weights,
+    taps, tall, wide, spectrum, mixed_out, mixed_in, conv_out, conv_in, gated,
+    taps_sem, here_sem, w_send, w_recv, in_send, in_recv, out_send, out_recv, g_send, g_recv,
+):
+    segs, chunks, chans, tokens = key.shape
+    groups = gathered.shape[0]
+    share = gathered.shape[-1]
+    outer = cos_t.shape[0]
+    slabs = tokens // lane_width
+    step = slabs + 8
+    tall_step = outer + 8
+    block = 8
+    s = lax.axis_index("seg")
+    h = lax.axis_index("ch")
+
+    def seg_peer(d):
+        return lax.rem(s + d, segs)
+
+    def ch_peer(d):
+        return lax.rem(h + d, groups)
+
+    fetch = pltpu.make_async_copy(kernel.at[s], taps, taps_sem)
+    fetch.start()
+    barrier = pltpu.get_barrier_semaphore()
+    for d in range(1, segs):
+        pl.semaphore_signal(barrier, inc=1, device_id=(seg_peer(d), h), device_id_type=MESH)
+    for d in range(1, groups):
+        pl.semaphore_signal(barrier, inc=1, device_id=(s, ch_peer(d)), device_id_type=MESH)
+    pl.semaphore_wait(barrier, segs + groups - 2)
+
+    def lanes(j):
+        return pl.ds(pl.multiple_of(j * lane_width, lane_width), lane_width)
+
+    def send_in(k, d):
+        return pltpu.make_async_remote_copy(
+            src_ref=mixed_out.at[k, d], dst_ref=mixed_in.at[k, s],
+            send_sem=in_send.at[k, d], recv_sem=in_recv.at[k, d],
+            device_id=(seg_peer(d), h), device_id_type=MESH,
+        )
+
+    def send_out(k, d):
+        return pltpu.make_async_remote_copy(
+            src_ref=conv_out.at[k, seg_peer(d)], dst_ref=conv_in.at[k, s],
+            send_sem=out_send.at[k, d], recv_sem=out_recv.at[k, d],
+            device_id=(seg_peer(d), h), device_id_type=MESH,
+        )
+
+    def send_gated(k, d):
+        peer = ch_peer(d)
+        part = pl.ds(pl.multiple_of(peer * share, lane_width), share)
+        return pltpu.make_async_remote_copy(
+            src_ref=gated.at[k, :, :, part], dst_ref=gathered.at[h, :, k],
+            send_sem=g_send.at[k, d], recv_sem=g_recv.at[k, d],
+            device_id=(s, peer), device_id_type=MESH,
+        )
+
+    def send_weight(d):
+        return pltpu.make_async_remote_copy(
+            src_ref=weight, dst_ref=weights.at[h],
+            send_sem=w_send.at[d], recv_sem=w_recv.at[d],
+            device_id=(s, ch_peer(d)), device_id_type=MESH,
+        )
+
+    for k in range(chunks):
+        for d in far_first(segs):
+            peer = seg_peer(d)
+
+            def mix(j, carry):
+                both = key[peer, k, :, lanes(j)].astype(f32) * value[peer, k, :, lanes(j)].astype(f32)
+                wide[pl.ds(j, chans, stride=step), :] = both
+                return carry
+
+            lax.fori_loop(0, slabs, mix, 0, unroll=4)
+            into = mixed_out.at[k, d] if d else mixed_in.at[k, s]
+            for i in range(chans):
+                into[i] = wide[i * step : i * step + slabs, :].astype(bf16)
+            if d:
+                send_in(k, d).start()
+        if k == 0:
+            for d in range(1, groups):
+                send_weight(d).start()
+    own_weight = pltpu.make_async_copy(weight, weights.at[h], here_sem.at[chunks])
+    own_weight.start()
+
+    fetch.wait()
+    for k in range(chunks):
+
+        def spread(j, carry):
+            tall[pl.ds(j, chans, stride=tall_step), :] = taps[k, :, lanes(j)]
+            return carry
+
+        lax.fori_loop(0, outer, spread, 0, unroll=4)
+        for at in range(0, chans, block):
+            signal = [
+                tall[i * tall_step : i * tall_step + outer, :].astype(bf16)
+                for i in range(at, at + block)
+            ]
+            out = forward(signal, first[...], inner[...], cos_t[...], sin_t[...])
+            spectrum[k, at : at + block] = out.astype(bf16).reshape(block, outer, 2 * lane_width)
+
+    for k in range(chunks):
+        for d in range(1, segs):
+            send_in(k, d).wait_recv()
+
+        for at in range(0, chans, block):
+            signal = [mixed_in[k, :, i].reshape(outer, lane_width) for i in range(at, at + block)]
+            filt = spectrum[k, at : at + block].reshape(block * outer, 2 * lane_width)
+            tables = (first[...], last[...], inner[...], inner_back[...], cos_t[...], sin_t[...])
+            parts = convolve_block(tables, signal, filt)
+            for i in range(block):
+                conv_out[k, :, at + i] = parts[i].reshape(segs, slabs, lane_width)
+        for d in far_first(segs):
+            if d:
+                send_out(k, d).start()
+
+    own_gated = []
+    for k in range(chunks):
+        for d in range(segs):
+            peer = seg_peer(d)
+            if d:
+                peer = lax.rem(s + segs - d, segs)
+                send_out(k, d).wait_recv()
+            source = conv_in.at[k, peer] if d else conv_out.at[k, s]
+            for i in range(chans):
+                wide[i * step : i * step + slabs, :] = source[i].astype(f32)
+            gain = skip[peer, k]
+
+            def combine(j, carry):
+                conv = wide[pl.ds(j, chans, stride=step), :]
+                both = key[peer, k, :, lanes(j)].astype(f32) * value[peer, k, :, lanes(j)].astype(f32)
+                total = gate[peer, k, :, lanes(j)].astype(f32) * (conv + gain * both)
+                gated[k, peer, :, lanes(j)] = total.astype(bf16)
+                return carry
+
+            lax.fori_loop(0, slabs, combine, 0, unroll=4)
+        for d in range(1, groups):
+            send_gated(k, d).start()
+        part = pl.ds(pl.multiple_of(h * share, lane_width), share)
+        own = pltpu.make_async_copy(gated.at[k, :, :, part], gathered.at[h, :, k], here_sem.at[k])
+        own.start()
+        own_gated.append(own)
+
+    for d in range(1, groups):
+        send_weight(d).wait()
+    own_weight.wait()
+    for k in range(chunks):
+        for d in range(1, segs):
+            send_in(k, d).wait_send()
+            send_out(k, d).wait_send()
+        for d in range(1, groups):
+            send_gated(k, d).wait()
+        own_gated[k].wait()
+
+
+def far_first(segs):
+    return [d for d in range(segs - 1, 0, -1)] + [0]
+
+
+def whole_layer(gate_in, key_in, value_in, kernel, skip_gain, out_weight, chans):
+    segs, groups = lax.axis_size("seg"), lax.axis_size("ch")
+    channels, tokens = key_in.shape
+    full_len = kernel.shape[1]
+    outer = full_len // lane_width
+    slabs = tokens // lane_width
+    features = out_weight.shape[1]
+    chunks = channels // segs // chans
+    share = tokens // groups
+    tables = make_tables(outer)
+    split = (segs, chunks, chans)
+    args = (
+        *tables,
+        key_in.reshape(*split, tokens),
+        value_in.reshape(*split, tokens),
+        gate_in.reshape(*split, tokens),
+        skip_gain.reshape(*split, 1),
+        kernel.reshape(*split, full_len),
+        out_weight,
+    )
+    vmem = pl.BlockSpec(memory_space=pltpu.VMEM)
+    hbm = pl.BlockSpec(memory_space=pl.ANY)
+    piece = pltpu.VMEM((chunks, segs, chans, slabs, lane_width), bf16)
+    dma = pltpu.SemaphoreType.DMA
+    gathered, weights = pl.pallas_call(
+        layer_kernel,
+        in_specs=[vmem] * 10 + [hbm, vmem],
+        out_specs=[hbm, hbm],
+        out_shape=[
+            jax.ShapeDtypeStruct((groups, segs, chunks, chans, share), bf16),
+            jax.ShapeDtypeStruct((groups, channels, features), bf16),
+        ],
+        scratch_shapes=[
+            pltpu.VMEM((chunks, chans, full_len), f32),
+            pltpu.VMEM((chans * (outer + 8), lane_width), f32),
+            pltpu.VMEM((chans * (slabs + 8), lane_width), f32),
+            pltpu.VMEM((chunks, chans, outer, 2 * lane_width), bf16),
+            piece, piece, piece, piece,
+            pltpu.VMEM((chunks, segs, chans, tokens), bf16),
+            dma, dma((chunks + 1,)),
+            dma((groups,)), dma((groups,)),
+            dma((chunks, segs)), dma((chunks, segs)), dma((chunks, segs)), dma((chunks, segs)),
+            dma((chunks, groups)), dma((chunks, groups)),
+        ],
+        compiler_params=pltpu.CompilerParams(
+            collective_id=0, has_side_effects=True, vmem_limit_bytes=56 * 1024 * 1024
+        ),
+        name="layer",
+    )(*args)
+    result = lax.dot_general(
+        gathered.reshape(groups * channels, share),
+        weights.reshape(groups * channels, features),
+        (((0,), (0,)), ((), ())),
+        preferred_element_type=f32,
+    )
+    return result.astype(bf16)
+
+
 def on_device(gate_in, key_in, value_in, kernel, skip_gain, out_weight):
     seg_count = lax.axis_size("seg")
     seg_index = lax.axis_index("seg")
@@ -149,6 +381,9 @@
     outer = full_len // lane_width
     tables = make_tables(outer)
     col_count = channels // seg_count
+    sublanes = 16
+    if col_count % sublanes == 0 and tokens // lax.axis_size("ch") % lane_width == 0:
+        return whole_layer(gate_in, key_in, value_in, kernel, skip_gain, out_weight, sublanes)
     mixed = key_in.astype(f32) * value_in.astype(f32)
     mixed_sent = mixed.astype(bf16).reshape(channels, tokens // lane_width, lane_width)
     col_mixed = lax.all_to_all(mixed_sent, "seg", split_axis=0, concat_axis=1, tiled=True)

time: 150 us -> 98.4 us (0.66)
  Pallas kernels: 14.6 us -> 86.3 us
  blocking collectives: 63.4 us -> 0 us
  waiting for transfers between devices: 23.5 us -> 0 us
  between operations: 13.5 us -> 0.02 us
  local copies, waits for them, and re-layouts: 12 us -> 1.52 us
  starting transfers between devices: 6.35 us -> 0 us
  other arithmetic: 9.75 us -> 3.78 us
    pallas_call x2 -> x1, Pallas kernels: 14.6 us -> 86.3 us  [whole_layer(): pl.pallas_call(layer_kernel, in_specs=[vmem] * 10 + [hbm, vmem], out_spec...]
    all_to_all x2 -> x0, blocking collectives: 63.4 us -> none  [the longest x1 39 us: on_device(): lax.all_to_all(col_conv, 'seg', split_axis=1, concat_axis=0, tiled=True)]
    all_to_all x1 -> x0, waiting for transfers between devices: 22.8 us -> none  [on_device(): lax.all_to_all(mixed_sent, 'seg', split_axis=0, concat_axis=1, tiled=True)]
    unnamed x11 -> x0, local copies, waits for them, and re-layouts: 6.84 us -> none
    all_to_all x1 -> x0, starting transfers between devices: 6.35 us -> none  [on_device(): lax.all_to_all(mixed_sent, 'seg', split_axis=0, concat_axis=1, tiled=True)]
    convert_element_type x2 -> x0, other arithmetic: 3.61 us -> none  [the longest x1 3.35 us: on_device(): (gate_in.astype(f32) * (conv + skip_gain[:, None] * mixed)).astype(bf16)]
    pallas_call x1 -> x0, local copies, waits for them, and re-layouts: 2.42 us -> none  [convolve(): pl.pallas_call(conv_kernel, grid=(count // block,), in_specs=[whole(a) fo...]
    unnamed x1 -> x0, other arithmetic: 2.36 us -> none
  transfers between devices with their start and end apart: 2 -> 0, of which waited for: 1 -> 0; matrix products, arithmetic and copies ran while one was open for 14% -> 0% of each run, Pallas kernels for 10% -> 0%
where the time goes in v2:
time: 98.4 us; the launch traced here: 98.2 us
  Pallas kernels  86.3 us (88%)
  matrix products  6.6 us (7%)
  other arithmetic  3.78 us (4%)
  local copies, waits for them, and re-layouts  1.52 us (2%)
    pallas_call x1, Pallas kernels, whole_layer(): pl.pallas_call(layer_kernel, in_specs=[vmem] * 10 + [hbm, vmem], out_spec...  86.3 us
    dot_general x1, matrix products, whole_layer(): lax.dot_general(gathered.reshape(groups * channels, share), weights.resha...  6.6 us

profile of v2, /device:TPU:0, one launch (start us, length us, event | category | flops | bytes accessed | tf_op | source)
XLA Modules:
  0.0 98.2 jit_solution(13730051608762290062)
XLA Ops:
  0.0 0.3 negate_convert_fusion
  0.4 1.5 %reshape.35.skip = f32[4,3,16,1]{3,2,1,0:T(8,128)} reshape(f32[192]{0:T(256)} %param.10) | data formatting | bytes 1536 | tf_op jit(solution)/shard_map/reshape | solution.py:334
  1.9 0.7 fusion.1
  2.6 1.5 %fusion.29 = (f32[128,128]{1,0:T(8,128)}, bf16[128,128]{1,0:T(8,128)(2,1)S(1)}, bf16[128,128]{1,0:T(8,128)(2,1)S(1)}, f32[128,128]{1,0:T(8,128)S(1)}, f32[128,128]{1,0:T(8,128)S(1)}, /*index=5*/f32[128,128]{1,0:T(8,128)}) fusion(s32[128]{0:T(128)S(1)} %broadcast_add_fusion), kind=kLoop, calls=%fused_computation.53 | loop fusion | flops 688128 | bytes 328192 | tf_op jit(solution)/shard_map/sin | solution.py:19
  4.1 0.6 pad_maximum_fusion.4.first
  4.7 0.6 fusion.2.last
  5.3 86.3 %layer.1 = (bf16[8,4,3,16,512]{4,3,2,1,0:T(8,128)(2,1)}, bf16[8,192,1536]{2,1,0:T(8,128)(2,1)}) custom-call(bf16[256,128]{1,0:T(8,128)(2,1)} %pad_maximum_fusion.4.first, bf16[128,256]{1,0:T(8,128)(2,1)} %fusion.2.last, bf16[256,256]{1,0:T(8,128)(2,1)} %get-tuple-element.10.inner, bf16[256,256]{1,0:T(8,128)(2,1)} %get-tuple-element.9.inner_back, ...), custom_call_target="tpu_custom_call" | custom-call | tf_op jit(solution)/shard_map/layer/pallas_call | solution.py:342
  91.6 6.6 %convolution_convert_fusion = bf16[512,1536]{1,0:T(8,128)(2,1)} fusion(bf16[1536,512]{1,0:T(8,128)(2,1)} %bitcast.13, bf16[1536,1536]{1,0:T(8,128)(2,1)} %bitcast.12), kind=kOutput, calls=%fused_computation | convolution fusion | flops 2416705536 | bytes 7864320 | tf_op jit(solution)/shard_map/dot_general | solution.py:367
  (2 shorter events, 0.0 us)

commit v3 on v2

--- a/solution.py
+++ b/solution.py
@@ -3,6 +3,7 @@
 
 import jax
 import jax.numpy as jnp
+import numpy as np
 from jax import lax
 from jax.experimental import pallas as pl
 from jax.experimental.pallas import tpu as pltpu
@@ -14,23 +15,23 @@
 
 
 def angles(rows, cols, period):
-    product = rows[:, None] * cols[None, :] % (4 * period)
-    theta = product.astype(f32) * (2.0 * math.pi / (4 * period))
-    return jnp.cos(theta), jnp.sin(theta)
+    theta = (rows[:, None] * cols[None, :] % (4 * period)) * (2.0 * math.pi / (4 * period))
+    return np.cos(theta), np.sin(theta)
 
 
 def make_tables(outer):
-    quarter = 4 * jnp.arange(outer, dtype=jnp.int32) + 1
-    row = jnp.arange(outer, dtype=jnp.int32)
-    lane = jnp.arange(lane_width, dtype=jnp.int32)
+    quarter = 4 * np.arange(outer) + 1
+    row = np.arange(outer)
+    lane = np.arange(lane_width)
     cos_o, sin_o = angles(quarter, row, outer)
     cos_t, sin_t = angles(quarter, lane, outer * lane_width)
     cos_i, sin_i = angles(4 * lane, lane, lane_width)
-    first = jnp.concatenate([cos_o, -sin_o], axis=0).astype(bf16)
-    last = (jnp.concatenate([cos_o.T, -sin_o.T], axis=1) / (outer * lane_width)).astype(bf16)
-    inner = jnp.block([[cos_i, -sin_i], [sin_i, cos_i]]).astype(bf16)
-    inner_back = jnp.block([[cos_i, sin_i], [-sin_i, cos_i]]).astype(bf16)
-    return first, last, inner, inner_back, cos_t, sin_t
+    first = np.concatenate([cos_o, -sin_o], axis=0)
+    last = np.concatenate([cos_o.T, -sin_o.T], axis=1) / (outer * lane_width)
+    inner = np.block([[cos_i, -sin_i], [sin_i, cos_i]])
+    inner_back = np.block([[cos_i, sin_i], [-sin_i, cos_i]])
+    narrow = [jnp.asarray(m.astype(np.float32).astype(bf16)) for m in (first, last, inner, inner_back)]
+    return (*narrow, jnp.asarray(cos_t.astype(np.float32)), jnp.asarray(sin_t.astype(np.float32)))
 
 
 def forward(signal, first, inner, cos_t, sin_t):
@@ -158,7 +159,7 @@
 def layer_kernel(
     first, last, inner, inner_back, cos_t, sin_t, key, value, gate, skip, kernel, weight,
     gathered, weights,
-    taps, tall, wide, spectrum, mixed_out, mixed_in, conv_out, conv_in, gated,
+    gains, taps, tall, wide, spectrum, mixed_out, mixed_in, conv_out, conv_in, gated,
     taps_sem, here_sem, w_send, w_recv, in_send, in_recv, out_send, out_recv, g_send, g_recv,
 ):
     segs, chunks, chans, tokens = key.shape
@@ -241,6 +242,12 @@
     own_weight = pltpu.make_async_copy(weight, weights.at[h], here_sem.at[chunks])
     own_weight.start()
 
+    for g in range(segs):
+        for k in range(chunks):
+            for i in range(chans):
+                level = skip[(g * chunks + k) * chans + i]
+                gains[g, k, i : i + 1, :] = jnp.full((1, lane_width), level, f32)
+
     fetch.wait()
     for k in range(chunks):
 
@@ -282,7 +289,7 @@
             source = conv_in.at[k, peer] if d else conv_out.at[k, s]
             for i in range(chans):
                 wide[i * step : i * step + slabs, :] = source[i].astype(f32)
-            gain = skip[peer, k]
+            gain = gains[peer, k]
 
             def combine(j, carry):
                 conv = wide[pl.ds(j, chans, stride=step), :]
@@ -331,7 +338,7 @@
         key_in.reshape(*split, tokens),
         value_in.reshape(*split, tokens),
         gate_in.reshape(*split, tokens),
-        skip_gain.reshape(*split, 1),
+        skip_gain,
         kernel.reshape(*split, full_len),
         out_weight,
     )
@@ -341,13 +348,14 @@
     dma = pltpu.SemaphoreType.DMA
     gathered, weights = pl.pallas_call(
         layer_kernel,
-        in_specs=[vmem] * 10 + [hbm, vmem],
+        in_specs=[vmem] * 9 + [pl.BlockSpec(memory_space=pltpu.SMEM), hbm, vmem],
         out_specs=[hbm, hbm],
         out_shape=[
             jax.ShapeDtypeStruct((groups, segs, chunks, chans, share), bf16),
             jax.ShapeDtypeStruct((groups, channels, features), bf16),
         ],
         scratch_shapes=[
+            pltpu.VMEM((segs, chunks, chans, lane_width), f32),
             pltpu.VMEM((chunks, chans, full_len), f32),
             pltpu.VMEM((chans * (outer + 8), lane_width), f32),
             pltpu.VMEM((chans * (slabs + 8), lane_width), f32),
@@ -381,7 +389,7 @@
     outer = full_len // lane_width
     tables = make_tables(outer)
     col_count = channels // seg_count
-    sublanes = 16
+    sublanes = 8
     if col_count % sublanes == 0 and tokens // lax.axis_size("ch") % lane_width == 0:
         return whole_layer(gate_in, key_in, value_in, kernel, skip_gain, out_weight, sublanes)
     mixed = key_in.astype(f32) * value_in.astype(f32)

time: 98.4 us -> 90.7 us (0.922)
  other arithmetic: 3.78 us -> 0 us
  Pallas kernels: 86.3 us -> 83.9 us
  local copies, waits for them, and re-layouts: 1.52 us -> 0 us
    pallas_call x1, Pallas kernels: 86.3 us -> 83.9 us  [whole_layer(): pl.pallas_call(layer_kernel, in_specs=[vmem] * 9 + [pl.BlockSpec(memory_s...]
    reshape x1 -> x0, local copies, waits for them, and re-layouts: 1.52 us -> none  [whole_layer(): skip_gain.reshape(*split, 1)]
    sin x1 -> x0, other arithmetic: 1.45 us -> none  [angles(): return (jnp.cos(theta), jnp.sin(theta))]
    concatenate x2 -> x0, other arithmetic: 1.35 us -> none  [the longest x1 0.72 us: make_tables(): inner_back = jnp.block([[cos_i, sin_i], [-sin_i, cos_i]]).astype(bf16)]
where the time goes in v3:
time: 90.7 us; the launch traced here: 90.6 us
  Pallas kernels  83.9 us (93%)
  matrix products  6.6 us (7%)
    pallas_call x1, Pallas kernels, whole_layer(): pl.pallas_call(layer_kernel, in_specs=[vmem] * 9 + [pl.BlockSpec(memory_s...  83.9 us
    dot_general x1, matrix products, whole_layer(): lax.dot_general(gathered.reshape(groups * channels, share), weights.resha...  6.6 us

profile of v3, /device:TPU:0, one launch (start us, length us, event | category | flops | bytes accessed | tf_op | source)
XLA Modules:
  0.0 90.6 jit_solution(11259649337286161761)
XLA Ops:
  0.0 83.9 %layer.1 = (bf16[8,4,6,8,512]{4,3,2,1,0:T(8,128)(2,1)}, bf16[8,192,1536]{2,1,0:T(8,128)(2,1)}) custom-call(bf16[256,128]{1,0:T(8,128)(2,1)} %constant.12.clone.first, bf16[128,256]{1,0:T(8,128)(2,1)} %constant.13.clone.last, bf16[256,256]{1,0:T(8,128)(2,1)} %constant.14.clone.inner, bf16[256,256]{1,0:T(8,128)(2,1)} %constant.15.clone.inner_back, ...), custom_call_target="tpu_custom_call" | custom-call | tf_op jit(solution)/shard_map/layer/pallas_call | solution.py:349
  84.0 6.6 %convolution_convert_fusion = bf16[512,1536]{1,0:T(8,128)(2,1)} fusion(bf16[1536,512]{1,0:T(8,128)(2,1)} %bitcast.13, bf16[1536,1536]{1,0:T(8,128)(2,1)} %bitcast.12), kind=kOutput, calls=%fused_computation | convolution fusion | flops 2416705536 | bytes 7864320 | tf_op jit(solution)/shard_map/dot_general | solution.py:375
